TPU v7x, 256 devices: a whole 4x4x8 slice. The times are simulated.
256 devices in a mesh: zero: 16 (over y, x), model: 8 (over z), copy: 2 (over core).
Axes of the slice: x: 4, y: 4, z: 8, core: 2. Of those that a mesh axis runs over, the one named last changes fastest.
Arguments:
- train_query: float32 [10240, 5120], P(('copy', 'zero'), 'model'), parts along dimension 0, may hold values from -0.125 to 0.125
- slow_query: float32 [10240, 5120], P(('copy', 'zero'), 'model'), parts along dimension 0, may hold values from -0.078125 to 0.078125
- train_key: float32 [10240, 5120], P(('copy', 'zero'), 'model'), parts along dimension 0, may hold values from -0.125 to 0.125
- slow_key: float32 [10240, 5120], P(('copy', 'zero'), 'model'), parts along dimension 0, may hold values from -0.078125 to 0.078125
- train_value: float32 [10240, 5120], P(('copy', 'zero'), 'model'), parts along dimension 0, may hold values from -0.125 to 0.125
- slow_value: float32 [10240, 5120], P(('copy', 'zero'), 'model'), parts along dimension 0, may hold values from -0.078125 to 0.078125
- norm_train: float32 [10240], P(('copy', 'zero', 'model')), parts along dimension 0, may hold values from 0.25 to 1.75
- norm_step: float32 [10240], P(('copy', 'zero', 'model')), parts along dimension 0, may hold values from -0.3 to 0.3
Outputs:
- final_query: bfloat16 [10240, 5120], P('copy', 'model'), parts along dimension 0
- final_key: bfloat16 [10240, 5120], P('copy', 'model'), parts along dimension 0
- final_value: bfloat16 [10240, 5120], P('copy', 'model'), parts along dimension 0
- scale_query: float32 [10240], P(('copy', 'model')), parts along dimension 0
- scale_key: float32 [10240], P(('copy', 'model')), parts along dimension 0
- scale_value: float32 [10240], P(('copy', 'model')), parts along dimension 0
- serve_norm: bfloat16 [10240], P('copy'), parts along dimension 0
- result_query: float32 [10240, 5120], P(('copy', 'zero'), 'model'), parts along dimension 0
- result_key: float32 [10240, 5120], P(('copy', 'zero'), 'model'), parts along dimension 0
- result_value: float32 [10240, 5120], P(('copy', 'zero'), 'model'), parts along dimension 0
There are 2 independent parts, one for each index of `copy`. A program takes and returns all parts, laid end to end along the dimension named above; each array names one. Nothing has to cross between parts.
All inputs are finite; a program needn't handle non-finite values.
Results may differ from a plain program's by a relative error of at most 0.001.
Values may be sent and summed in bfloat16 or wider, within the bound.
A program may use at most 128 MiB of HBM per device.

v0:
```python
import jax
import jax.numpy as jnp
from jax import lax
from jax.sharding import Mesh
from jax.sharding import PartitionSpec as P

ZERO = ("zero_0", "zero_1")
ZERO_MODEL = ("zero_0", "zero_1", "model")
COPY_ZERO = ("copy", "zero_0", "zero_1")
COPY_ZERO_MODEL = ("copy", "zero_0", "zero_1", "model")


keep_rate = 0.75


def from_everyone(shard, axis):
    count = lax.axis_size(axis)
    return lax.all_to_all(
        jnp.broadcast_to(shard[None], (count, *shard.shape)), axis, 0, 0, tiled=True
    )


def of_everyone(shard, axis):
    return from_everyone(shard, axis).sum(axis=0)


def in_one(arrays, axis):
    line, at, finished = (jnp.concatenate([a.reshape(-1) for a in arrays]), 0, [])
    running = of_everyone(line, axis)
    for a in arrays:
        finished.append(running[at : at + a.size].reshape(a.shape))
        at += a.size
    return tuple(finished)


def sent_together(arrays, axis, dim, along):
    ends, at = ([], 0)
    for a in arrays[:-1]:
        at += a.shape[along]
        ends.append(at)
    both = jnp.concatenate(arrays, axis=along)
    return tuple(jnp.split(lax.all_gather(both, axis, axis=dim, tiled=True), ends, axis=along))


def in_order(tiles, dim):
    shape = list(tiles.shape[1:])
    shape[dim] *= tiles.shape[0]
    return jnp.moveaxis(tiles, 0, dim).reshape(shape)


def gather_in_order(shard, axes, order):
    tiles = shard
    for k in order:
        tiles = lax.all_gather(tiles, axes[k])
    done = order[::-1]
    back = [done.index(k) for k in range(len(axes))]
    tiles = tiles.transpose(*back, *range(len(axes), tiles.ndim))
    return tiles.reshape(-1, *shard.shape)


def gather_axes(shard, axes, order, dim):
    return in_order(gather_in_order(shard, axes, order), dim)


def body(
    train_query, slow_query, train_key, slow_key, train_value, slow_value, norm_train, norm_step
):
    result_query = keep_rate * slow_query + (1.0 - keep_rate) * train_query
    result_key = keep_rate * slow_key + (1.0 - keep_rate) * train_key
    result_value = keep_rate * slow_value + (1.0 - keep_rate) * train_value
    total_query, total_key, total_value = in_one(
        (
            jnp.sum(result_query * result_query, axis=0),
            jnp.sum(result_key * result_key, axis=0),
            jnp.sum(result_value * result_value, axis=0),
        ),
        ZERO,
    )
    scale_query = jnp.sqrt(total_query)
    scale_key = jnp.sqrt(total_key)
    scale_value = jnp.sqrt(total_value)
    narrow_query, narrow_key, narrow_value = (
        (result_query / scale_query).astype(jnp.bfloat16),
        (result_key / scale_key).astype(jnp.bfloat16),
        (result_value / scale_value).astype(jnp.bfloat16),
    )
    final_query, final_key, final_value = sent_together(
        (narrow_query, narrow_key, narrow_value), ZERO, 0, 1
    )
    serve_norm = gather_axes(
        (norm_train + norm_step).astype(jnp.bfloat16), ZERO_MODEL, (0, 1, 2), 0
    )
    return (
        final_query,
        final_key,
        final_value,
        scale_query,
        scale_key,
        scale_value,
        serve_norm,
        result_query,
        result_key,
        result_value,
    )


def solution(mesh):
    torus = Mesh(
        mesh.devices.reshape(4, 4, mesh.shape["model"], mesh.shape["copy"]),
        ("zero_0", "zero_1", "model", "copy"),
    )
    return jax.shard_map(
        body,
        mesh=torus,
        in_specs=(
            P(COPY_ZERO, "model"),
            P(COPY_ZERO, "model"),
            P(COPY_ZERO, "model"),
            P(COPY_ZERO, "model"),
            P(COPY_ZERO, "model"),
            P(COPY_ZERO, "model"),
            P(COPY_ZERO_MODEL),
            P(COPY_ZERO_MODEL),
        ),
        out_specs=(
            P("copy", "model"),
            P("copy", "model"),
            P("copy", "model"),
            P(("copy", "model")),
            P(("copy", "model")),
            P(("copy", "model")),
            P("copy"),
            P(COPY_ZERO, "model"),
            P(COPY_ZERO, "model"),
            P(COPY_ZERO, "model"),
        ),
        check_vma=False,
    )
```

profile of v0, /device:TPU:32, one launch (start us, length us, event | category | flops | bytes accessed | tf_op | source)
XLA Modules:
  0.0 179.3 jit_solution(5986251678206804639)
XLA Ops:
  7.2 0.0 all-gather.6.cloned.1.call-start
  7.3 1.7 multiply_reduce_fusion.2
  9.0 0.1 copy-done.4
  9.1 0.2 copy-done.5
  9.3 1.7 multiply_reduce_fusion
  11.1 0.0 copy-start
  11.1 0.1 broadcast_in_dim.2
  11.2 14.8 %all_to_all.6 = f32[16,1,1920]{2,1,0:T(1,128)S(1)} all-to-all(f32[16,1,1920]{2,1,0:T(1,128)S(1)} %broadcast_in_dim.2), channel_id=1, replica_groups=mesh['zero_0'=4,'zero_1'=4,'model'=8,'copy'=2] {'zero_0','zero_1'}, dimensions={0} | all-to-all | bytes 245760 | tf_op jit(solution)/shard_map/all_to_all | solution.py:18
  25.9 0.1 reduce_sum.39
  26.1 0.0 copy-start.6
  26.1 0.1 divide_convert_fusion.1
  26.2 0.1 divide_convert_fusion
  26.3 0.1 divide_convert_fusion.2
  26.4 1.1 pad_maximum_fusion
  27.5 0.0 all-gather.6.cloned.1.call-update
  27.6 0.6 dynamic-slice
  28.8 0.2 dynamic-update-slice
  29.1 8.6 %all-reduce = bf16[160]{0:T(256)(128)(2,1)S(1)} all-reduce(bf16[160]{0:T(256)(128)(2,1)S(1)} %dynamic-update-slice), channel_id=2, replica_groups=mesh['zero_0'=4,'zero_1'=4,'model'=8,'copy'=2] {'zero_0'}, use_global_device_ids=true, to_apply=%add | all-reduce | flops 160 | bytes 640
  37.7 0.1 reshape.35
  37.8 8.4 %all-gather.3 = bf16[4,4,40]{2,1,0:T(4,128)(2,1)S(1)} all-gather(bf16[1,4,40]{2,1,0:T(4,128)(2,1)S(1)} %reshape.35), channel_id=3, replica_groups=mesh['zero_0'=4,'zero_1'=4,'model'=8,'copy'=2] {'zero_1'}, dimensions={0}, use_global_device_ids=true | all-gather | bytes 1600 | tf_op jit(solution)/shard_map/all_gather | solution.py:54
  46.1 27.5 %all-gather.2 = bf16[32,4,40]{2,1,0:T(4,128)(2,1)S(1)} all-gather(bf16[4,4,40]{2,1,0:T(4,128)(2,1)S(1)} %all-gather.3), channel_id=4, replica_groups=mesh['zero_0'=4,'zero_1'=4,'model'=8,'copy'=2] {'model'}, dimensions={0}, use_global_device_ids=true | all-gather | bytes 11520 | tf_op jit(solution)/shard_map/all_gather | solution.py:54
  73.7 0.7 reshape_reshape.3
  74.4 83.1 %all-gather.6.cloned.1.call-done = bf16[5120,1920]{1,0:T(8,128)(2,1)} async-done(((bf16[320,1920]{1,0:T(8,128)(2,1)}), bf16[5120,1920]{1,0:T(8,128)(2,1)}) %all-gather.6.cloned.1.call-update) | async-done | bytes 19660816 | tf_op jit(solution)/shard_map/all_gather | solution.py:42
  157.5 14.9 %fusion = (bf16[5120,640]{1,0:T(8,128)(2,1)}, bf16[5120,640]{1,0:T(8,128)(2,1)}, bf16[5120,640]{1,0:T(8,128)(2,1)}) fusion(bf16[5120,1920]{1,0:T(8,128)(2,1)} %all-gather.6.cloned.1.call-done), kind=kLoop, calls=%fused_computation.15 | loop fusion | bytes 39321600 | tf_op jit(solution)/shard_map/split | solution.py:42
  (26 shorter events, 0.1 us)
Async XLA Ops:
  7.2 1.8 copy-start.3
  7.2 150.3 %all-gather.6.cloned.1.call-start = ((), (), s32[]{:S(2)}) async-start(), calls=%async_computation.1 | async-start | bytes 20889600 | tf_op jit(solution)/shard_map/all_gather | solution.py:42
  7.2 1.8 %copy-start.4 = (f32[320,640]{1,0:T(8,128)S(1)}, f32[320,640]{1,0:T(8,128)}, u32[]{:S(2)}) copy-start(f32[320,640]{1,0:T(8,128)} %param.13) | copy-start | bytes 2457604
  7.2 2.1 %copy-start.5 = (f32[320,640]{1,0:T(8,128)S(1)}, f32[320,640]{1,0:T(8,128)}, u32[]{:S(2)}) copy-start(f32[320,640]{1,0:T(8,128)} %param.10) | copy-start | bytes 2457604
  9.3 16.9 %copy-start.2 = (f32[320,640]{1,0:T(8,128)}, f32[320,640]{1,0:T(8,128)S(1)}, u32[]{:S(2)}) copy-start(f32[320,640]{1,0:T(8,128)S(1)} %get-tuple-element.11) | copy-start | bytes 2457604
  11.1 16.4 %copy-start = (f32[320,640]{1,0:T(8,128)}, f32[320,640]{1,0:T(8,128)S(1)}, u32[]{:S(2)}) copy-start(f32[320,640]{1,0:T(8,128)S(1)} %get-tuple-element.15) | copy-start | bytes 2457604
  11.1 16.4 %copy-start.1 = (f32[320,640]{1,0:T(8,128)}, f32[320,640]{1,0:T(8,128)S(1)}, u32[]{:S(2)}) copy-start(f32[320,640]{1,0:T(8,128)S(1)} %get-tuple-element.23) | copy-start | bytes 2457604
  26.1 1.4 copy-start.6
  26.1 1.4 copy-start.7
  26.1 1.4 copy-start.8
  26.3 1.3 copy-start.11
  26.3 2.5 %copy-start.9 = (f32[40]{0:T(128)S(1)}, f32[40]{0:T(128)}, u32[]{:S(2)}) copy-start(f32[40]{0:T(128)} %param.14) | copy-start | bytes 484
  26.3 2.5 %copy-start.10 = (f32[40]{0:T(128)S(1)}, f32[40]{0:T(128)}, u32[]{:S(2)}) copy-start(f32[40]{0:T(128)} %param.15) | copy-start | bytes 484
Sparse Core Ops, SparseCore 0:
  27.7 129.8 all-gather.5
where the time goes:
time: 181 us; the launch traced here: 179 us
  waiting for transfers between devices  83.2 us (46%)
  blocking collectives  59.3 us (33%)
  local copies, waits for them, and re-layouts  17.1 us (9%)
  between operations  14.9 us (8%)
  other arithmetic  4.85 us (3%)
    all_gather x1, waiting for transfers between devices, sent_together(): lax.all_gather(both, axis, axis=dim, tiled=True)  83.1 us
    all_gather x2, blocking collectives, gather_in_order(): tiles = lax.all_gather(tiles, axes[k])  35.9 us
    split x1, local copies, waits for them, and re-layouts, sent_together(): jnp.split(lax.all_gather(both, axis, axis=dim, tiled=True), ends, axis=al...  14.9 us
    all_to_all x1, blocking collectives, from_everyone(): lax.all_to_all(jnp.broadcast_to(shard[None], (count, *shard.shape)), axis...  14.8 us
    unnamed x1, blocking collectives  8.59 us
  transfers between devices with their start and end apart: 1, of which 1 were waited for; matrix products, arithmetic and copies ran while one was open for 1% of the time, Pallas kernels for 0%

commit v1 on v0

v1 whole, which is shorter than its diff:
```python
import functools

import jax
import jax.numpy as jnp
from jax import lax
from jax.experimental import pallas as pl
from jax.experimental.pallas import tpu as pltpu
from jax.sharding import Mesh
from jax.sharding import PartitionSpec as P

COPY_ZERO = ("copy", "zero_0", "zero_1")
COPY_ZERO_MODEL = ("copy", "zero_0", "zero_1", "model")
MESH = pl.DeviceIdType.MESH

KEEP_RATE = 0.75
SIDE = 4
PLANE = SIDE * SIDE
DEPTH = 8
LINKS = (("zero_1", 1), ("zero_1", -1), ("zero_0", 1), ("zero_0", -1))
WINDOW = 384
EARLY = {"zero_1": (8, 32), "zero_0": (24, 16)}


ORDER = (
    ("own 1", None), ("own 0", None), ("side 1", 0), ("pass", None), ("side 1", -1), ("side 1", 1), ("side 1", 2),
    ("side 0", None), ("side pass", None),
)
FIRST = 3
NEXT = {0: 3, 1: 4, 2: 5, 3: 6, 4: 7, 6: 8}


def place(here, link, kind, across, arrived):
    axis, step = LINKS[link]
    along = (-step if "pass" in kind else 0) - (step if arrived else 0)
    at = lax.rem(here[axis] + along + 2 * SIDE, SIDE)
    if "side" in kind:
        unit = link ^ 2 if kind != "side 0" else link ^ 3
        other = "zero_0" if axis == "zero_1" else "zero_1"
        beside = slice(None) if across is None else lax.rem(here[other] + across + SIDE, SIDE)
        return (beside, at, unit) if axis == "zero_1" else (at, beside, unit)
    unit = link ^ 1 if kind == "own 0" else link
    return (here["zero_0"], at, unit) if axis == "zero_1" else (at, here["zero_1"], unit)


def work(
    train_q, slow_q, train_k, slow_k, train_v, slow_v, gain_train, gain_step,
    out, result, scale_q, scale_k, scale_v, gain,
    train, slow, early, sums_x, sums_y, gains, gain_z, gain_plane, gain_rows,
    load_sem, gain_sem, early_send, early_recv, sum_send, sum_recv, z_send, z_recv, plane_send, plane_recv,
    link_send, link_recv, ready,
):
    rows, width = train_q.shape
    unit = rows // 4
    columns = [slice(w * width, (w + 1) * width) for w in range(3)]
    x, y, z = lax.axis_index("zero_1"), lax.axis_index("zero_0"), lax.axis_index("model")
    me = y * SIDE + x
    here = {"zero_1": x, "zero_0": y}

    def near(axis, step):
        return {axis: lax.rem(here[axis] + step + SIDE, SIDE)}

    def deep(step):
        return lax.rem(z + step + DEPTH, DEPTH)

    barrier = pltpu.get_barrier_semaphore()
    friends = [near(axis, step) for axis in ("zero_1", "zero_0") for step in (1, 2, 3)]
    for friend in friends:
        pl.semaphore_signal(barrier, inc=1, device_id=friend, device_id_type=MESH)

    top = DEPTH - 1
    lower = (z + top) // DEPTH + (z + 1) // DEPTH

    def greet(sem, step):
        pl.semaphore_signal(sem, inc=1, device_id={"model": deep(step)}, device_id_type=MESH)

    pl.when(z < top)(lambda: greet(barrier, 1))
    pl.when(z == 0)(lambda: greet(barrier, -1))

    ahead = [sum(EARLY[axis]) for axis, _ in LINKS]
    first = [EARLY[axis][0] for axis, _ in LINKS]
    spans = [(u * unit, first[u]) for u in range(4)] + [(u * unit + first[u], unit - first[u]) for u in range(4)]
    loads = []
    for n, (start, size) in enumerate(spans):
        at = pl.ds(start, size)
        group = []
        for w, (t, s) in enumerate(((train_q, slow_q), (train_k, slow_k), (train_v, slow_v))):
            group.append(pltpu.make_async_copy(t.at[at, :], train.at[at, columns[w]], load_sem.at[n, w, 0]))
            group.append(pltpu.make_async_copy(s.at[at, :], slow.at[at, columns[w]], load_sem.at[n, w, 1]))
        for c in group:
            c.start()
        loads.append(group)
    gain_loads = [
        pltpu.make_async_copy(gain_train, gains.at[0], gain_sem.at[0]),
        pltpu.make_async_copy(gain_step, gains.at[1], gain_sem.at[1]),
    ]
    for c in gain_loads:
        c.start()

    def average(n):
        for c in loads[n]:
            c.wait()
        start, size = spans[n]
        r = KEEP_RATE * slow[start : start + size, :] + (1.0 - KEEP_RATE) * train[start : start + size, :]
        result[start : start + size, :] = r
        return jnp.sum((r * r).reshape(size // 8, 8, 3 * width), axis=0)

    def early_copy(link, half):
        axis, step = LINKS[link]
        first, second = EARLY[axis]
        start, size = (0, first) if half == 0 else (first, second)
        return pltpu.make_async_remote_copy(
            src_ref=result.at[pl.ds(link * unit + start, size), :], dst_ref=early.at[link, pl.ds(start, size), :],
            send_sem=early_send.at[link, half], recv_sem=early_recv.at[link, half],
            device_id=near(axis, step), device_id_type=MESH,
        )

    square = average(0)
    for n in range(1, 4):
        square = square + average(n)
    pl.semaphore_wait(barrier, len(friends) + lower)
    for link in range(4):
        early_copy(link, 0).start()
    for n in range(4, 8):
        square = square + average(n)

    def ring(ref, index, axis, send, recv):
        copies = []
        for step in (1, 2, 3):
            copies.append(pltpu.make_async_remote_copy(
                src_ref=ref.at[index], dst_ref=ref.at[index], send_sem=send.at[step - 1], recv_sem=recv.at[step - 1],
                device_id=near(axis, step), device_id_type=MESH,
            ))
            copies[-1].start()
        return copies

    def landed(ref, axis, send, recv):
        for step in (1, 2, 3):
            index = near(axis, -step)[axis]
            pltpu.make_async_remote_copy(
                src_ref=ref.at[index], dst_ref=ref.at[index], send_sem=send.at[step - 1], recv_sem=recv.at[step - 1],
                device_id=near(axis, step), device_id_type=MESH,
            ).wait_recv()

    sums_x[x] = jnp.sum(square, axis=0, keepdims=True)
    sent = ring(sums_x, x, "zero_1", sum_send.at[0], sum_recv.at[0])
    for link in (0, 1):
        early_copy(link, 1).start()

    pl.when(z > 0)(lambda: greet(ready, -1))
    pl.when(z == top)(lambda: greet(ready, 1))

    for c in gain_loads:
        c.wait()
    value = (gains[0] + gains[1]).astype(jnp.bfloat16)
    count = gain_train.shape[1]
    put = (
        lax.broadcasted_iota(jnp.int32, (count, WINDOW), 1)
        == lax.broadcasted_iota(jnp.int32, (count, WINDOW), 0) + (lax.rem(me, 2) * 64 + z * count)
    )
    gain_z[z] = jnp.dot(value, jnp.where(put, 1.0, 0.0).astype(jnp.bfloat16), preferred_element_type=jnp.float32)

    landed(sums_x, "zero_1", sum_send.at[0], sum_recv.at[0])
    sums_y[y] = (sums_x[0] + sums_x[1]) + (sums_x[2] + sums_x[3])
    sent += ring(sums_y, y, "zero_0", sum_send.at[1], sum_recv.at[1])
    for link in (2, 3):
        early_copy(link, 1).start()
    landed(sums_y, "zero_0", sum_send.at[1], sum_recv.at[1])
    root = jnp.sqrt((sums_y[0] + sums_y[1]) + (sums_y[2] + sums_y[3]))
    inverse = 1.0 / root

    def normalise(link, start, size):
        out[y, x, link, pl.ds(start, size), :] = (
            result[link * unit + start : link * unit + start + size, :] * inverse
        ).astype(jnp.bfloat16)

    def piece(link, k, arrived):
        kind, across = ORDER[k]
        block = place(here, link, kind, across, arrived)
        start = ahead[link] if kind == "own 1" else 0
        return out.at[(*block, pl.ds(start, unit - start))]

    def copy(link, k, arrived):
        ref = piece(link, k, arrived)
        return pltpu.make_async_remote_copy(
            src_ref=ref, dst_ref=ref, send_sem=link_send.at[link, k], recv_sem=link_recv.at[link, k],
            device_id=near(*LINKS[link]), device_id_type=MESH,
        )

    for link in range(4):
        normalise(link, ahead[link], unit - ahead[link])
        copy(link, 0, False).start()
    for link in range(4):
        normalise(link, 0, ahead[link])
    for k in range(1, FIRST):
        for link in range(4):
            copy(link, k, False).start()
    for w, ref in enumerate((scale_q, scale_k, scale_v)):
        ref[...] = root[0, columns[w]]

    for link in range(4):
        axis, step = LINKS[link]
        for half in range(2):
            early_copy(link, half).wait_recv()
        at = {**here, **near(axis, -step)}
        out[at["zero_0"], at["zero_1"], link, pl.ds(0, ahead[link]), :] = (
            early[link, : ahead[link], :] * inverse
        ).astype(jnp.bfloat16)

    def hop(step, up, arrived):
        index = deep((1 - step if up else step - 1) + (0 if not arrived else -1 if up else 1))
        at = (0 if up else 4) + step - 1
        return pltpu.make_async_remote_copy(
            src_ref=gain_z.at[index], dst_ref=gain_z.at[index], send_sem=z_send.at[at], recv_sem=z_recv.at[at],
            device_id={"model": deep(1 if up else -1)}, device_id_type=MESH,
        )

    hops = [(step, up) for step in range(1, 5) for up in ((True, False) if step < 4 else (True,))]

    def gains_at(k):
        if k <= 4:
            for step, up in hops:
                if step == k:
                    hop(step, up, True).wait_recv()
            for step, up in hops:
                if step == k + 1:
                    hop(step, up, False).start()
        if k == 4:
            column = gain_z[0]
            for n in range(1, DEPTH):
                column = column + gain_z[n]
            gain_plane[y, x] = column
            return ring(gain_plane.at[y], x, "zero_1", plane_send.at[0], plane_recv.at[0])
        if k == 6:
            landed(gain_plane.at[y], "zero_1", plane_send.at[0], plane_recv.at[0])
            return ring(gain_plane, y, "zero_0", plane_send.at[1], plane_recv.at[1])
        if k == 8:
            landed(gain_plane, "zero_0", plane_send.at[1], plane_recv.at[1])
            for n in range(PLANE // 2):
                a, b = gain_plane[n // 2, n % 2 * 2], gain_plane[n // 2, n % 2 * 2 + 1]
                five = [a[:, :128], a[:, 128:256], a[:, 256:] + b[:, :128], b[:, 128:256], b[:, 256:]]
                for j in range(5):
                    gain_rows[n * 5 + j : n * 5 + j + 1, :] = five[j]
            gain[...] = gain_rows[...].astype(jnp.bfloat16)
        return []

    pl.when(z < top)(lambda: pl.semaphore_wait(ready, 2 - lower))
    sent += gains_at(0)
    for k in range(len(ORDER)):
        for link in range(4):
            copy(link, k, True).wait_recv()
        sent += gains_at(k + 1)
        for link in range(4):
            if k in NEXT:
                copy(link, NEXT[k], False).start()
    for c in sent:
        c.wait_send()
    for step, up in hops:
        hop(step, up, False).wait_send()
    for link in range(4):
        for half in range(2):
            early_copy(link, half).wait_send()
        for k in range(len(ORDER)):
            copy(link, k, False).wait_send()


def store(out, result, scale_q, scale_k, scale_v, gain, *rest):
    finals, scales, serve, results, sem = rest[0:3], rest[3:6], rest[6], rest[7:10], rest[10]
    width = finals[0].shape[-1]
    copies = []
    for w, scale in enumerate((scale_q, scale_k, scale_v)):
        columns = slice(w * width, (w + 1) * width)
        for part in range(2):
            at = pl.ds(part * SIDE // 2, SIDE // 2)
            copies.append((out.at[at, :, :, :, columns], finals[w].at[at]))
        copies.append((result.at[:, columns], results[w]))
        copies.append((scale, scales[w]))
    copies.append((gain, serve))
    started = [pltpu.make_async_copy(a, b, sem.at[n]) for n, (a, b) in enumerate(copies)]
    for c in started:
        c.start()
    for c in started:
        c.wait()


def body(*args):
    rows, width = args[0].shape
    f32, bf16 = jnp.float32, jnp.bfloat16
    hbm, vmem = pl.BlockSpec(memory_space=pltpu.HBM), pl.BlockSpec(memory_space=pltpu.VMEM)
    dma = pltpu.SemaphoreType.DMA
    gains = args[6].shape[0] * DEPTH * PLANE
    steps = len(ORDER)
    unit = rows // 4
    most = max(sum(v) for v in EARLY.values())
    args = [pltpu.with_memory_space_constraint(a, pltpu.HBM) for a in (*args[:6], args[6][None], args[7][None])]
    held = pl.pallas_call(
        work,
        out_shape=(
            pltpu.VMEM((SIDE, SIDE, 4, unit, 3 * width), bf16),
            pltpu.VMEM((rows, 3 * width), f32),
            *[pltpu.VMEM((width,), f32)] * 3,
            pltpu.VMEM((gains // 128, 128), bf16),
        ),
        in_specs=[hbm] * 8,
        out_specs=(vmem,) * 6,
        scratch_shapes=[
            pltpu.VMEM((rows, 3 * width), f32),
            pltpu.VMEM((rows, 3 * width), f32),
            pltpu.VMEM((4, most, 3 * width), f32),
            pltpu.VMEM((SIDE + 1, 1, 3 * width), f32),
            pltpu.VMEM((SIDE + 1, 1, 3 * width), f32),
            pltpu.VMEM((2 + 8, 1, args[6].shape[1]), f32),
            pltpu.VMEM((DEPTH + 3, 1, WINDOW), f32),
            pltpu.VMEM((SIDE + 1, SIDE, 1, WINDOW), f32),
            pltpu.VMEM((gains // 128, 128), f32),
            dma((8, 3, 2)), dma((2,)),
            dma((4, 2)), dma((4, 2)),
            dma((2, 3)), dma((2, 3)),
            dma((7,)), dma((7,)),
            dma((2, 3)), dma((2, 3)),
            dma((4, steps)), dma((4, steps)),
            pltpu.SemaphoreType.REGULAR,
        ],
        compiler_params=pltpu.CompilerParams(
            collective_id=0, has_side_effects=True, vmem_limit_bytes=20 << 20
        ),
        name="gather",
    )(*args)
    outs = pl.pallas_call(
        store,
        out_shape=(
            *[jax.ShapeDtypeStruct((SIDE, SIDE, 4, unit, width), bf16)] * 3,
            *[jax.ShapeDtypeStruct((width,), f32)] * 3,
            jax.ShapeDtypeStruct((gains // 128, 128), bf16),
            *[jax.ShapeDtypeStruct((rows, width), f32)] * 3,
        ),
        in_specs=[vmem] * 6,
        out_specs=(hbm,) * 10,
        scratch_shapes=[dma((13,))],
        compiler_params=pltpu.CompilerParams(vmem_limit_bytes=2 << 20),
        name="store",
    )(*held)
    finals = [f.reshape(PLANE * rows, width) for f in outs[:3]]
    return (*finals, *outs[3:6], outs[6].reshape(gains), *outs[7:])


def solution(mesh):
    torus = Mesh(
        mesh.devices.reshape(SIDE, SIDE, mesh.shape["model"], mesh.shape["copy"]),
        ("zero_0", "zero_1", "model", "copy"),
    )
    weight, whole = P(COPY_ZERO, "model"), P("copy", "model")
    return jax.shard_map(
        body,
        mesh=torus,
        in_specs=(weight,) * 6 + (P(COPY_ZERO_MODEL),) * 2,
        out_specs=(whole,) * 3 + (P(("copy", "model")),) * 3 + (P("copy"),) + (weight,) * 3,
        check_vma=False,
    )
```

time: 181 us -> 120 us (0.66)
  Pallas kernels: 0 us -> 119 us
  waiting for transfers between devices: 83.2 us -> 0 us
  blocking collectives: 59.3 us -> 0 us
  local copies, waits for them, and re-layouts: 17.1 us -> 0 us
  between operations: 14.9 us -> 0.65 us
  other arithmetic: 4.85 us -> 0 us
    pallas_call x0 -> x2, Pallas kernels: none -> 119 us  [the longest x1 111 us: body(): pl.pallas_call(work, out_shape=(pltpu.VMEM((SIDE, SIDE, 4, unit, 3 * widt...]
    all_gather x1 -> x0, waiting for transfers between devices: 83.1 us -> none  [sent_together(): lax.all_gather(both, axis, axis=dim, tiled=True)]
    all_gather x2 -> x0, blocking collectives: 35.9 us -> none  [gather_in_order(): tiles = lax.all_gather(tiles, axes[k])]
    split x1 -> x0, local copies, waits for them, and re-layouts: 14.9 us -> none  [sent_together(): jnp.split(lax.all_gather(both, axis, axis=dim, tiled=True), ends, axis=al...]
    all_to_all x1 -> x0, blocking collectives: 14.8 us -> none  [from_everyone(): lax.all_to_all(jnp.broadcast_to(shard[None], (count, *shard.shape)), axis...]
    unnamed x1 -> x0, blocking collectives: 8.59 us -> none
    reduce_sum x3 -> x0, other arithmetic: 3.51 us -> none  [the longest x1 1.73 us: body(): jnp.sum(result_value * result_value, axis=0)]
  transfers between devices with their start and end apart: 1 -> 0, of which waited for: 1 -> 0; matrix products, arithmetic and copies ran while one was open for 1% -> 0% of each run, Pallas kernels for 0% -> 0%
where the time goes in v1:
time: 120 us; the launch traced here: 119 us
  Pallas kernels  119 us (99%)
    pallas_call x1, Pallas kernels, body(): pl.pallas_call(work, out_shape=(pltpu.VMEM((SIDE, SIDE, 4, unit, 3 * widt...  111 us
    pallas_call x1, Pallas kernels, body(): pl.pallas_call(store, out_shape=(*[jax.ShapeDtypeStruct((SIDE, SIDE, 4, u...  7.61 us

profile of v1, /device:TPU:32, one launch (start us, length us, event | category | flops | bytes accessed | tf_op | source)
XLA Modules:
  0.0 119.4 jit_solution(7857463102588789108)
XLA Ops:
  0.6 111.1 %gather.1 = (bf16[4,4,4,80,1920]{4,3,2,1,0:T(8,128)(2,1)S(1)}, f32[320,1920]{1,0:T(8,128)S(1)}, f32[640]{0:T(1024)S(1)}, f32[640]{0:T(1024)S(1)}, f32[640]{0:T(1024)S(1)}, /*index=5*/bf16[40,128]{1,0:T(8,128)(2,1)S(1)}) custom-call(f32[320,640]{1,0:T(8,128)} %train_q.1, f32[320,640]{1,0:T(8,128)} %slow_q.1, f32[320,640]{1,0:T(8,128)} %train_k.1, ...), custom_call_target="tpu_custom_call" | custom-call | tf_op jit(solution)/shard_map/gather/pallas_call | solution.py:295
  111.8 7.6 %store.1 = (bf16[4,4,4,80,640]{4,3,2,1,0:T(8,128)(2,1)}, bf16[4,4,4,80,640]{4,3,2,1,0:T(8,128)(2,1)}, bf16[4,4,4,80,640]{4,3,2,1,0:T(8,128)(2,1)}, f32[640]{0:T(...) custom-call(bf16[4,4,4,80,1920]{4,3,2,1,0:T(8,128)(2,1)S(1)} %get-tu, ...), custom_call_target="tpu_custom_call" | custom-call | tf_op jit(solution)/shard_map/store/pallas_call | solution.py:328

commit v2 on v1

--- a/solution.py
+++ b/solution.py
@@ -188,6 +188,7 @@
 
     for link in range(4):
         normalise(link, ahead[link], unit - ahead[link])
+    for link in range(4):
         copy(link, 0, False).start()
     for link in range(4):
         normalise(link, 0, ahead[link])

time: 120 us -> 120 us (level)
  no operation moved by 1% of the time
where the time goes in v2:
time: 120 us; the launch traced here: 119 us
  Pallas kernels  119 us (99%)
    pallas_call x1, Pallas kernels, body(): pl.pallas_call(work, out_shape=(pltpu.VMEM((SIDE, SIDE, 4, unit, 3 * widt...  111 us
    pallas_call x1, Pallas kernels, body(): pl.pallas_call(store, out_shape=(*[jax.ShapeDtypeStruct((SIDE, SIDE, 4, u...  7.61 us

profile of v2, /device:TPU:32, one launch (start us, length us, event | category | flops | bytes accessed | tf_op | source)
XLA Modules:
  0.0 119.4 jit_solution(11962027471949015574)
XLA Ops:
  0.6 111.1 %gather.1 = (bf16[4,4,4,80,1920]{4,3,2,1,0:T(8,128)(2,1)S(1)}, f32[320,1920]{1,0:T(8,128)S(1)}, f32[640]{0:T(1024)S(1)}, f32[640]{0:T(1024)S(1)}, f32[640]{0:T(1024)S(1)}, /*index=5*/bf16[40,128]{1,0:T(8,128)(2,1)S(1)}) custom-call(f32[320,640]{1,0:T(8,128)} %train_q.1, f32[320,640]{1,0:T(8,128)} %slow_q.1, f32[320,640]{1,0:T(8,128)} %train_k.1, ...), custom_call_target="tpu_custom_call" | custom-call | tf_op jit(solution)/shard_map/gather/pallas_call | solution.py:296
  111.8 7.6 %store.1 = (bf16[4,4,4,80,640]{4,3,2,1,0:T(8,128)(2,1)}, bf16[4,4,4,80,640]{4,3,2,1,0:T(8,128)(2,1)}, bf16[4,4,4,80,640]{4,3,2,1,0:T(8,128)(2,1)}, f32[640]{0:T(...) custom-call(bf16[4,4,4,80,1920]{4,3,2,1,0:T(8,128)(2,1)S(1)} %get-tu, ...), custom_call_target="tpu_custom_call" | custom-call | tf_op jit(solution)/shard_map/store/pallas_call | solution.py:329
